TPU v7x, 32 devices: a whole 2x2x4 slice. The times are simulated.
32 devices in a mesh: section: 4 (over z), expert: 4 (over y, x), dp: 2 (over core).
Axes of the slice: x: 2, y: 2, z: 4, core: 2. Of those that a mesh axis runs over, the one named last changes fastest.
Arguments:
- stash: bfloat16 [4, 256, 2048], P('section', 'dp', 'expert'), may hold values from -6 to 6
- cotangent: bfloat16 [4, 256, 2048], P('section', 'dp', 'expert'), may hold values from -6 to 6
- backward_expert_routes: int32 [4, 256, 2], P('section', 'dp'), may hold values from 0 to 3, all different within a row; in each aligned block of 128 rows (0 to 127, 128 to 255, ..., all dimensions but the last counted through in order) at most 80 rows name the same one
- backward_job_lengths: int32 [4, 4], P('section'), may hold values from 1 to 128, 256 in all within a row
- layer_norm_gains: float32 [4, 2048], P('section'), may hold values from 0.25 to 1.75
- router: bfloat16 [4, 2048, 4], P('section'), may hold values from -0.125 to 0.125
- expert_gate_weight: bfloat16 [4, 2048, 28672], P('section', None, ('expert', 'dp')), may hold values from -0.125 to 0.125
- expert_up_weight: bfloat16 [4, 2048, 28672], P('section', None, ('expert', 'dp')), may hold values from -0.125 to 0.125
- expert_down_weight: bfloat16 [4, 28672, 2048], P('section', ('expert', 'dp')), may hold values from -0.0625 to 0.0625
- adapter_down_maps: bfloat16 [4, 2048, 64], P('section', 'expert'), may hold values from -0.125 to 0.125
- adapter_up_maps: bfloat16 [4, 64, 2048], P('section', None, 'expert'), may hold values from -1.5 to 1.5
Outputs:
- handed_back: bfloat16 [4, 256, 2048], P('section', 'dp', 'expert')
- grad_lora_down: float32 [4, 2048, 64], P('section', 'expert')
- grad_lora_up: float32 [4, 64, 2048], P('section', None, 'expert')
Inputs may be any that keep to these rules, and one draw needn't show every extreme that they name: `backward_expert_routes`: each row names two different experts. In each aligned block of 128 rows (the tokens of one device) no expert is named more than 80 times. `backward_job_lengths`: each row sums to 256.
All inputs are finite; a program needn't handle non-finite values.
Results may differ from a plain program's by a relative error of at most 0.008.
Values may be sent and summed in bfloat16 or wider, within the bound.
A program may use at most 128 MiB of HBM per device.

v0:
```python
import functools

import jax
import jax.numpy as jnp
from jax import lax
from jax.experimental import pallas as pl
from jax.experimental.pallas import tpu as pltpu
from jax.sharding import PartitionSpec as P

ADAPTER_RANK = 16
CAP = 80

EPS = 1e-05
ADAPTER_SCALE = 0.5
MESH = pl.DeviceIdType.MESH
VMEM_LIMIT = 60 * 1024 * 1024
LANES = 128
LAST = (((1,), (1,)), ((), ()))
FIRST = (((0,), (0,)), ((), ()))


def job_columns(job_token_lengths, offset, count):
    ends = jnp.cumsum(job_token_lengths, dtype=jnp.int32)
    position = offset + jnp.arange(count, dtype=jnp.int32)
    owner = jnp.sum((ends[None, :] <= position[:, None]).astype(jnp.int32), axis=1, dtype=jnp.int32)
    column_owner = (
        jnp.arange(job_token_lengths.shape[0] * ADAPTER_RANK, dtype=jnp.int32) // ADAPTER_RANK
    )
    return (owner[:, None] == column_owner[None, :]).astype(jnp.float32)


def greet(targets):
    barrier = pltpu.get_barrier_semaphore()
    for target in targets:
        pl.semaphore_signal(barrier, inc=1, device_id=target, device_id_type=MESH)
    pl.semaphore_wait(barrier, len(targets))


def gather_kernel(
    n, per, select_ref, x_ref, g_ref, gain_ref, route_ref, down_ref, up_ref,
    rows_out, stats_out, lows_out, rows_ref, stats_ref, lows_ref, rs, rr, ss, sr, ls, lr, fs, fr, own,
):
    me = lax.axis_index("expert")
    core = lax.axis_index("dp")
    partner = {"dp": 1 - core}
    peers = [lax.rem(me + k, n) for k in range(1, n)]
    greet([{"expert": peer} for peer in peers] + [partner])

    def send(src, dst, a, b, k, target):
        copy = pltpu.make_async_remote_copy(
            src_ref=src, dst_ref=dst, send_sem=a.at[k], recv_sem=b.at[k],
            device_id=target, device_id_type=MESH,
        )
        copy.start()
        return copy

    width = x_ref.shape[1]
    x, g = x_ref[...], g_ref[...]
    for e in range(select_ref.shape[0]):
        chosen = select_ref[e]
        rows_ref[e, :, :width] = jnp.dot(chosen, x, preferred_element_type=jnp.float32).astype(
            jnp.bfloat16
        )
        rows_ref[e, :, width:] = jnp.dot(chosen, g, preferred_element_type=jnp.float32).astype(
            jnp.bfloat16
        )
    rows, small = [], []
    for k, peer in enumerate(peers):
        target = {"expert": peer}
        rows.append(send(rows_ref.at[peer // per], rows_out.at[core, me], rs, rr, k, target))
    xf = x.astype(jnp.float32)
    gained = (xf * gain_ref[...]).astype(jnp.bfloat16)
    raw = lax.dot_general(route_ref[...], gained, LAST, preferred_element_type=jnp.float32)
    square = lax.dot_general(
        jnp.ones(route_ref.shape, jnp.float32), xf * xf, LAST,
        precision=lax.Precision.HIGHEST, preferred_element_type=jnp.float32,
    )
    line = lax.broadcasted_iota(jnp.int32, raw.shape, 0)
    stats_ref[...] = jnp.where(line == 0, square, raw)
    lows_ref[...] = jnp.concatenate(
        [
            jnp.dot(gained, down_ref[...], preferred_element_type=jnp.float32),
            lax.dot_general(g, up_ref[...], LAST, preferred_element_type=jnp.float32),
        ],
        axis=1,
    ).astype(jnp.bfloat16)
    for k, peer in enumerate(peers):
        target = {"expert": peer}
        small.append(send(stats_ref, stats_out.at[me], ss, sr, k, target))
        small.append(send(lows_ref, lows_out.at[me], ls, lr, k, target))
    mine = rows_ref.at[me // per]
    local = [
        pltpu.make_async_copy(mine, rows_out.at[core, me], own.at[0]),
        pltpu.make_async_copy(stats_ref, stats_out.at[me], own.at[1]),
        pltpu.make_async_copy(lows_ref, lows_out.at[me], own.at[2]),
    ]
    for copy in local:
        copy.start()
    passed = [send(mine, rows_out.at[core, me], fs, fr, n - 1, partner)]
    for k in range(n - 1):
        rows[k].wait_recv()
        origin = lax.rem(me + (n - 1 - k), n)
        landed = rows_out.at[core, origin]
        passed.append(send(landed, landed, fs, fr, k, partner))
    for copy in rows:
        copy.wait_send()
    for copy in small + local + passed:
        copy.wait()


def gather(n, per, shards, select, x, g, gain, route, down, up):
    count, width = x.shape
    rows = jax.ShapeDtypeStruct(select.shape[:2] + (2 * width,), x.dtype)
    stats = jax.ShapeDtypeStruct((route.shape[0], count), jnp.float32)
    lows = jax.ShapeDtypeStruct((count, 2 * down.shape[1]), x.dtype)
    vmem = pl.BlockSpec(memory_space=pltpu.VMEM)
    dma = pltpu.SemaphoreType.DMA
    return pl.pallas_call(
        functools.partial(gather_kernel, n, per),
        out_shape=(
            jax.ShapeDtypeStruct((shards, n) + rows.shape[1:], rows.dtype),
            jax.ShapeDtypeStruct((n,) + stats.shape, stats.dtype),
            jax.ShapeDtypeStruct((n,) + lows.shape, lows.dtype),
        ),
        in_specs=[vmem] * 7,
        out_specs=(vmem,) * 3,
        scratch_shapes=[pltpu.VMEM(a.shape, a.dtype) for a in (rows, stats, lows)] + [dma((n - 1,))] * 6 + [dma((n,))] * 2 + [dma((3,))],
        compiler_params=pltpu.CompilerParams(
            collective_id=0, has_side_effects=True, vmem_limit_bytes=VMEM_LIMIT
        ),
    )(select, x, g, gain, route, down, up)


def expert_kernel(
    n, width, rows_ref, gain_ref, wg_ref, wu_ref, wd_ref, dn_ref, vec_ref, normed, cot, acc, vec
):
    step = pl.program_id(0)
    shards, cap = rows_ref.shape[0], rows_ref.shape[2]

    @pl.when(step == 0)
    def _():
        for s in range(shards):
            r = slice(s * cap, (s + 1) * cap)
            total = jnp.zeros((cap, 1), jnp.float32)
            for j in range(n):
                x = rows_ref[s, j, :, :width].astype(jnp.float32)
                total += jnp.sum(x * x, axis=1, keepdims=True)
            scale = lax.rsqrt(total / (n * width) + EPS)
            for j in range(n):
                c = slice(j * width, (j + 1) * width)
                x = rows_ref[s, j, :, :width].astype(jnp.float32)
                normed[r, c] = (x * scale * gain_ref[:, c]).astype(jnp.bfloat16)
                cot[r, c] = rows_ref[s, j, :, width:]
        acc[...] = jnp.zeros_like(acc)
        vec[...] = jnp.zeros_like(vec)

    x, g = normed[...], cot[...]
    gate = jnp.dot(x, wg_ref[...], preferred_element_type=jnp.float32)
    up = jnp.dot(x, wu_ref[...], preferred_element_type=jnp.float32)
    back = lax.dot_general(g, wd_ref[...], LAST, preferred_element_type=jnp.float32)
    sig = jax.nn.sigmoid(gate)
    act = gate * sig
    d_up = back * act
    d_gate = back * up * sig * (1.0 + gate * (1.0 - sig))
    gate_term = jnp.sum(d_up * up, axis=1, keepdims=True)
    stat_term = jnp.sum(d_gate * gate + d_up * up, axis=1, keepdims=True)
    lane = lax.broadcasted_iota(jnp.int32, vec.shape, 1)
    vec[...] += jnp.where(lane % 2 == 0, gate_term, stat_term)
    acc[...] += lax.dot_general(
        d_gate.astype(jnp.bfloat16), wg_ref[...], LAST, preferred_element_type=jnp.float32
    ) + lax.dot_general(
        d_up.astype(jnp.bfloat16), wu_ref[...], LAST, preferred_element_type=jnp.float32
    )

    @pl.when(step == pl.num_programs(0) - 1)
    def _():
        for s in range(shards):
            r = slice(s * cap, (s + 1) * cap)
            vec_ref[s] = vec[r, :]
            for j in range(n):
                dn_ref[s, j] = acc[r, j * width:(j + 1) * width]


def expert_back(rows, gains, wg, wu, wd):
    shards, n, cap, double = rows.shape
    width = double // 2
    model, hidden = n * width, wg.shape[2]
    tile = next(t for t in (512, 256, 128, hidden) if hidden % t == 0)
    slots = shards * cap
    return pl.pallas_call(
        functools.partial(expert_kernel, n, width),
        grid=(hidden // tile,),
        out_shape=(
            jax.ShapeDtypeStruct((shards, n, cap, width), jnp.float32),
            jax.ShapeDtypeStruct((shards, cap, LANES), jnp.float32),
        ),
        in_specs=[
            pl.BlockSpec(rows.shape, lambda i: (0, 0, 0, 0)),
            pl.BlockSpec((1, model), lambda i: (0, 0)),
            pl.BlockSpec((None, model, tile), lambda i: (0, 0, i)),
            pl.BlockSpec((None, model, tile), lambda i: (0, 0, i)),
            pl.BlockSpec((None, tile, model), lambda i: (0, i, 0)),
        ],
        out_specs=(
            pl.BlockSpec((shards, n, cap, width), lambda i: (0, 0, 0, 0)),
            pl.BlockSpec((shards, cap, LANES), lambda i: (0, 0, 0)),
        ),
        scratch_shapes=[
            pltpu.VMEM((slots, model), jnp.bfloat16),
            pltpu.VMEM((slots, model), jnp.bfloat16),
            pltpu.VMEM((slots, model), jnp.float32),
            pltpu.VMEM((slots, LANES), jnp.float32),
        ],
        compiler_params=pltpu.CompilerParams(
            dimension_semantics=("arbitrary",), vmem_limit_bytes=VMEM_LIMIT
        ),
    )(rows, gains, wg, wu, wd)


def scatter_kernel(
    n, per, experts, sections,
    dn_ref, vec_ref, select_ref, tok_ref, lows_ref, mask_ref, x_ref, g_ref, gain_ref, rt_ref,
    down_ref,
    back_out, pd_out, pu_out,
    pd_ref, pu_ref, pdn, pvec, ppd, ppu, sendbuf, landing, result, ps, pr, qs, qr, es, er, zs, zr,
):
    me = lax.axis_index("expert")
    core = lax.axis_index("dp")
    sec = lax.axis_index("section")
    other = 1 - core
    partner = {"dp": other}
    width = x_ref.shape[1]
    ahead = {"section": lax.rem(sec + sections - 1, sections)}
    behind = {"section": lax.rem(sec + 1, sections)}
    peers = [lax.rem(me + k, n) for k in range(1, n)]
    greet([{"expert": peer} for peer in peers] + [partner, ahead, behind])

    def send(src, dst, a, b, k, target):
        copy = pltpu.make_async_remote_copy(
            src_ref=src, dst_ref=dst, send_sem=a.at[k], recv_sem=b.at[k],
            device_id=target, device_id_type=MESH,
        )
        copy.start()
        return copy

    shared = [send(vec_ref.at[other], pvec, qs, qr, 0, partner)]
    blocks = [
        send(dn_ref.at[other, peer], pdn.at[k], ps, pr, k, partner)
        for k, peer in enumerate(peers + [me])
    ]
    shared[0].wait()
    v = vec_ref[core] + pvec[...]
    high = v.astype(jnp.bfloat16)
    rest = (v - high.astype(jnp.float32)).astype(jnp.bfloat16)
    lane = lax.broadcasted_iota(jnp.int32, v.shape, 1)
    packed = jnp.where(lane < 2, high.astype(jnp.float32), rest.astype(jnp.float32)).astype(
        jnp.bfloat16
    )
    sent = []
    for k, peer in enumerate(peers):
        blocks[k].wait()
        sendbuf[k, :, :width] = (dn_ref[core, peer] + pdn[k]).astype(jnp.bfloat16)
        sendbuf[k, :, width:] = packed
        sent.append(send(sendbuf.at[k], landing.at[k], es, er, k, {"expert": peer}))
    blocks[n - 1].wait()
    own_rows = (dn_ref[core, me] + pdn[n - 1]).astype(jnp.bfloat16)

    token = tok_ref[...]
    column = lambda i: token[:, i:i + 1]
    scale = column(2 * experts + 1)
    x = x_ref[...].astype(jnp.float32)
    ranks = down_ref.shape[1]
    low_all = lows_ref[0].astype(jnp.float32)
    for j in range(1, n):
        low_all = low_all + lows_ref[j].astype(jnp.float32)
    raw_low, g_low = low_all[:, :ranks], low_all[:, ranks:]
    mask = mask_ref[...]
    low = (raw_low * scale * mask).astype(jnp.bfloat16)
    d_low = (ADAPTER_SCALE * g_low * mask).astype(jnp.bfloat16)
    normed = (x * scale * gain_ref[...]).astype(jnp.bfloat16)
    pd_ref[...] = lax.dot_general(normed, d_low, FIRST, preferred_element_type=jnp.float32)
    pu_ref[...] = ADAPTER_SCALE * lax.dot_general(
        low, g_ref[...], FIRST, preferred_element_type=jnp.float32
    )
    shared.append(send(pd_ref, ppd, qs, qr, 1, partner))
    shared.append(send(pu_ref, ppu, qs, qr, 2, partner))
    low_stat = jnp.sum(d_low.astype(jnp.float32) * raw_low, axis=1, keepdims=True)
    spread = jnp.zeros_like(column(0))
    stat = jnp.zeros_like(spread)
    total = lax.dot_general(d_low, down_ref[...], LAST, preferred_element_type=jnp.float32)

    def pick(ref_index, values):
        return lax.dot_general(
            select_ref[ref_index], values, FIRST, preferred_element_type=jnp.float32
        )

    def weights_of(expert):
        gate, sign = jnp.zeros_like(spread), jnp.zeros_like(spread)
        for e in range(experts):
            mark = (expert == e).astype(jnp.float32)
            gate += mark * column(e)
            sign += mark * column(experts + e)
        return gate, sign

    def add(expert, row_part, vec_part, total, spread, stat):
        gate, sign = weights_of(expert)
        picked = pick(expert, vec_part)
        spread = spread + sign * (picked[:, 0:1] + picked[:, 2:3])
        stat = stat + gate * (picked[:, 1:2] + picked[:, 3:4])
        return total + gate * pick(expert, row_part), spread, stat

    total, spread, stat = add(me // per, own_rows, packed, total, spread, stat)
    for k in range(n - 1):
        sent[k].wait()
        expert = lax.rem(me + (n - 1 - k), n) // per
        total, spread, stat = add(
            expert, landing[k, :, :width], landing[k, :, width:], total, spread, stat
        )
    delta = spread * column(2 * experts)
    for e in range(experts):
        total = total + (delta * column(experts + e)) * rt_ref[e + 1:e + 2, :].astype(
            jnp.float32
        )
    stat = stat / scale + low_stat + delta * column(2 * experts + 2)
    g = g_ref[...].astype(jnp.float32)
    weighted = total * gain_ref[...]
    out = g + scale * weighted - x * (scale * scale * scale * stat / (n * width))
    result[...] = out.astype(jnp.bfloat16)
    handed = send(result, back_out, zs, zr, 0, ahead)
    shared[1].wait()
    pd_out[...] = pd_ref[...] + ppd[...]
    shared[2].wait()
    pu_out[...] = pu_ref[...] + ppu[...]
    handed.wait()


def scatter(n, per, experts, sections, dn, vec, *rest):
    cap, width = dn.shape[2:]
    x, down = rest[4], rest[8]
    pd = jax.ShapeDtypeStruct(down.shape, jnp.float32)
    pu = jax.ShapeDtypeStruct(down.shape[::-1], jnp.float32)
    vmem = pl.BlockSpec(memory_space=pltpu.VMEM)
    dma = pltpu.SemaphoreType.DMA
    return pl.pallas_call(
        functools.partial(scatter_kernel, n, per, experts, sections),
        out_shape=(
            jax.ShapeDtypeStruct(x.shape, jnp.bfloat16),
            jax.ShapeDtypeStruct(pd.shape, jnp.float32),
            jax.ShapeDtypeStruct(pu.shape, jnp.float32),
        ),
        in_specs=[vmem] * (2 + len(rest)),
        out_specs=(vmem,) * 3,
        scratch_shapes=[
            pltpu.VMEM(pd.shape, jnp.float32),
            pltpu.VMEM(pu.shape, jnp.float32),
            pltpu.VMEM((n, cap, width), jnp.float32),
            pltpu.VMEM(vec.shape[1:], jnp.float32),
            pltpu.VMEM(pd.shape, jnp.float32),
            pltpu.VMEM(pu.shape, jnp.float32),
            pltpu.VMEM((n - 1, cap, width + LANES), jnp.bfloat16),
            pltpu.VMEM((n - 1, cap, width + LANES), jnp.bfloat16),
            pltpu.VMEM(x.shape, jnp.bfloat16),
            dma((n,)), dma((n,)), dma((3,)), dma((3,)),
            dma((n - 1,)), dma((n - 1,)), dma((1,)), dma((1,)),
        ],
        compiler_params=pltpu.CompilerParams(
            collective_id=1, has_side_effects=True, vmem_limit_bytes=VMEM_LIMIT
        ),
    )(dn, vec, *rest)


def body(
    stash,
    cotangent,
    backward_expert_routes,
    backward_job_lengths,
    layer_norm_gains,
    router,
    expert_gate_weight,
    expert_up_weight,
    expert_down_weight,
    adapter_down_maps,
    adapter_up_maps,
):
    n = lax.axis_size("expert")
    shards = lax.axis_size("dp")
    sections = lax.axis_size("section")
    experts = router.shape[2]
    per = n // experts
    me = lax.axis_index("expert")
    x, g = stash[0], cotangent[0]
    count, width = x.shape
    routes = backward_expert_routes[0]
    gain = lax.dynamic_slice_in_dim(layer_norm_gains, me * width, width, 1)
    route_cols = lax.dynamic_slice_in_dim(router[0], me * width, width, 0)
    down, up_map = adapter_down_maps[0], adapter_up_maps[0]
    ranks = down.shape[1]

    labels = jnp.arange(experts, dtype=jnp.int32)
    first = (routes[:, 0:1] == labels[None, :]).astype(jnp.float32)
    second = (routes[:, 1:2] == labels[None, :]).astype(jnp.float32)
    member = first + second
    order = jnp.arange(count, dtype=jnp.int32)
    before = (order[None, :] < order[:, None]).astype(jnp.bfloat16)
    rank = jnp.dot(before, member.astype(jnp.bfloat16), preferred_element_type=jnp.float32)
    place = jnp.where(member > 0, rank, -1.0)
    slots = jnp.arange(CAP, dtype=jnp.float32)
    select = (place.T[:, None, :] == slots[None, :, None]).astype(jnp.bfloat16)

    route_t = jnp.pad(route_cols.T, ((1, -(1 + experts) % 8), (0, 0)))

    all_rows, all_stats, all_lows = gather(
        n, per, shards, select, x, g, gain, route_t, down, up_map
    )

    dn, vec = expert_back(
        all_rows, layer_norm_gains, expert_gate_weight, expert_up_weight, expert_down_weight
    )

    stat = jnp.sum(all_stats, axis=0).T
    scale = lax.rsqrt(stat[:, 0:1] / (n * width) + EPS)
    raw_logits = stat[:, 1:1 + experts]
    sign = first - second
    raw_spread = jnp.sum(sign * raw_logits, axis=1, keepdims=True)
    upper = jax.nn.sigmoid(raw_spread * scale)
    table = upper * first + (1.0 - upper) * second
    mask = job_columns(backward_job_lengths[0], lax.axis_index("dp") * count, count)
    columns = [table, sign, upper * (1.0 - upper), scale, raw_spread]
    used = sum(c.shape[1] for c in columns)
    token = jnp.concatenate(columns + [jnp.zeros((count, -used % LANES), jnp.float32)], axis=1)

    handed_back, down_grad, up_grad = scatter(
        n, per, experts, sections, dn, vec, select, token, all_lows, mask, x, g, gain, route_t,
        down,
    )
    return (handed_back[None], down_grad[None], up_grad[None])


def solution(mesh):
    return jax.shard_map(
        body,
        mesh=mesh,
        in_specs=(
            P("section", "dp", "expert"),
            P("section", "dp", "expert"),
            P("section", "dp", None),
            P("section", None),
            P("section", None),
            P("section", None, None),
            P("section", None, ("expert", "dp")),
            P("section", None, ("expert", "dp")),
            P("section", ("expert", "dp"), None),
            P("section", "expert", None),
            P("section", None, "expert"),
        ),
        out_specs=(
            P("section", "dp", "expert"),
            P("section", "expert", None),
            P("section", None, "expert"),
        ),
        check_vma=False,
    )
```

profile of v0, /device:TPU:0, one launch (start us, length us, event | category | flops | bytes accessed | tf_op | source)
XLA Modules:
  0.0 74.8 jit_solution(5880057725753399901)
XLA Ops:
  0.6 0.0 copy-start
  0.6 0.8 %slice_bitcast_fusion.1 = (s32[128]{0:T(128)S(1)}, s32[128]{0:T(128)S(1)}) fusion(s32[128,2]{0,1:T(2,128)} %bitcast.33), kind=kLoop, calls=%fused_computation.33 | loop fusion | bytes 2048 | tf_op jit(solution)/shard_map/eq | solution.py:400
  1.4 0.2 convolution_select_fusion
  1.7 0.7 fusion.select_ref
  2.3 1.3 %constant_dynamic-slice_fusion.gain_ref = f32[1,512]{1,0:T(1,128)} fusion(f32[1,2048]{1,0:T(1,128)} %gain_ref.1, s32[]{:T(128)S(6)} %select_n.19), kind=kLoop, calls=%fused_computation.31 | loop fusion | bytes 4100 | tf_op jit(solution)/shard_map/dynamic_slice | solution.py:394
  3.6 0.0 copy-done
  3.6 0.6 pad.4.route_ref.rt_ref
  4.2 1.6 %copy.32 = bf16[1,512,64]{2,1,0:T(8,128)(2,1)} copy(bf16[1,512,64]{1,2,0:T(8,128)(2,1)} %param.20) | data formatting | bytes 131072 | tf_op args[9]
  5.8 16.8 %shard_map.130 = (bf16[2,4,80,1024]{3,2,1,0:T(8,128)(2,1)}, f32[4,8,128]{2,1,0:T(8,128)}, bf16[4,128,128]{2,1,0:T(8,128)(2,1)}) custom-call(bf16[4,80,128]{2,1,0:T(8,128)(2,1)} %fusion.select_ref, bf16[128,512]{1,0:T(8,128)(2,1)} %bitcast.24, bf16[128,512]{1,0:T(8,128)(2,1)} %bitcast.26, f32[1,512]{1,0:T(1,128)} %constant_dynamic-slice_fusion.gain_ref, ...), custom_call_target="tpu_custom_call" | custom-call | tf_op jit(solution)/shard_map/pallas_call | solution.py:118
  22.6 0.0 copy-start.1
  22.6 0.0 copy-start.2
  22.6 26.4 %shard_map.131 = (f32[2,4,80,512]{3,2,1,0:T(8,128)}, f32[2,80,128]{2,1,0:T(8,128)}) custom-call(bf16[2,4,80,1024]{3,2,1,0:T(8,128)(2,1)} %get-tuple-element.11.rows_ref, f32[1,2048]{1,0:T(1,128)} %gain_ref.1, bf16[1,2048,3584]{2,1,0:T(8,128)(2,1)} %wg_ref.1, bf16[1,2048,3584]{2,1,0:T(8,128)(2,1)} %wu_ref.1, bf16[1,3584,2048]{2,1,0:T(8,128)(2,1)} %wd_ref.1), custom_call_target="tpu_custom_call" | custom-call | tf_op jit(solution)/shard_map/pallas_call | solution.py:190
  49.1 0.0 copy-done.1
  49.1 0.1 copy.33
  49.2 0.2 fusion.4
  49.4 0.1 copy.34
  49.6 0.1 fusion.8
  49.7 0.1 convert_subtract_fusion
  49.9 0.8 %concatenate.3.tok_ref = f32[128,128]{1,0:T(8,128)} concatenate(f32[128,4]{1,0:T(8,128)S(1)} %get-tuple-element.40, f32[128,4]{1,0:T(8,128)S(1)} %get-tuple-element.39, f32[128,1]{1,0:T(8,128)S(1)} %get-tuple-element.36, f32[128,1]{1,0:T(8,128)S(1)} %get-tuple-element.38, f32[128,1]{1,0:T(8,128)S(1)} %copy.34, f32[128,117]{1,0:T(8,128)S(1)} %broadcast_in_dim.16), dimensions={1} | concatenate | bytes 131072 | tf_op jit(solution)/shard_map/concatenate | solution.py:430
  50.6 0.0 copy-done.2
  50.6 0.2 reduce-window.8
  50.8 0.1 convert_reduce_fusion
  50.9 0.7 compare_convert_fusion.mask_ref
  51.6 18.4 %shard_map.132 = (bf16[128,512]{1,0:T(8,128)(2,1)}, f32[512,64]{1,0:T(8,128)}, f32[64,512]{1,0:T(8,128)}) custom-call(f32[2,4,80,512]{3,2,1,0:T(8,128)} %get-tuple-element.12.dn_ref, f32[2,80,128]{2,1,0:T(8,128)} %get-tuple-element.13.vec_ref, bf16[4,80,128]{2,1,0:T(8,128)(2,1)} %fusion.select_ref, f32[128,128]{1,0:T(8,128)} %concatenate.3.tok_ref, ...), custom_call_target="tpu_custom_call" | custom-call | tf_op jit(solution)/shard_map/pallas_call | solution.py:344
  70.0 1.7 %copy.39 = f32[1,512,64]{1,2,0:T(8,128)} copy(f32[1,512,64]{2,1,0:T(8,128)} %bitcast.28) | data formatting | bytes 262144
  71.7 1.6 %copy.42 = bf16[1,128,512]{2,1,0:T(8,128)(2,1)} copy(bf16[1,128,512]{2,1,0:T(8,128)(2,1)} %bitcast.30) | data formatting | bytes 262144
  73.3 1.6 %copy.43 = f32[1,64,512]{2,1,0:T(8,128)} copy(f32[1,64,512]{2,1,0:T(8,128)} %bitcast.29) | data formatting | bytes 262144
  (6 shorter events, 0.1 us)
Async XLA Ops:
  0.6 3.0 %copy-start = (bf16[1,2048,4]{1,2,0:T(4,128)(2,1)S(1)}, bf16[1,2048,4]{1,2,0:T(4,128)(2,1)}, u32[]{:S(2)}) copy-start(bf16[1,2048,4]{1,2,0:T(4,128)(2,1)} %param.16) | copy-start | bytes 49156
  22.6 26.5 %copy-start.1 = (f32[4,8,128]{2,1,0:T(8,128)S(1)}, f32[4,8,128]{2,1,0:T(8,128)}, u32[]{:S(2)}) copy-start(f32[4,8,128]{2,1,0:T(8,128)} %get-tuple-element.14) | copy-start | bytes 49156
  22.6 28.0 %copy-start.2 = (s32[1,4]{1,0:T(1,128)S(1)}, s32[1,4]{1,0:T(1,128)}, u32[]{:S(2)}) copy-start(s32[1,4]{1,0:T(1,128)} %param.14) | copy-start | bytes 52
where the time goes:
time: 75.2 us; the launch traced here: 74.8 us
  Pallas kernels  61.6 us (82%)
  local copies, waits for them, and re-layouts  10.1 us (13%)
  other arithmetic  2.15 us (3%)
    pallas_call x1, Pallas kernels, expert_back(): pl.pallas_call(functools.partial(expert_kernel, n, width), grid=(hidden /...  26.4 us
    pallas_call x1, Pallas kernels, scatter(): pl.pallas_call(functools.partial(scatter_kernel, n, per, experts, section...  18.4 us
    pallas_call x1, Pallas kernels, gather(): pl.pallas_call(functools.partial(gather_kernel, n, per), out_shape=(jax.S...  16.8 us
    unnamed x10, local copies, waits for them, and re-layouts  6.47 us

commit v1 on v0

v1 whole, which is shorter than its diff:
```python
import functools

import jax
import jax.numpy as jnp
from jax import lax
from jax.experimental import pallas as pl
from jax.experimental.pallas import tpu as pltpu
from jax.sharding import PartitionSpec as P

CAP = 80

EPS = 1e-05
ADAPTER_SCALE = 0.5
MESH = pl.DeviceIdType.MESH
VMEM_LIMIT = 67_043_328
LANES = 128
DEPTH = 2
TILES = (1792, 896, 512, 256, 128)
LAST = (((1,), (1,)), ((), ()))
FIRST = (((0,), (0,)), ((), ()))


def greet(targets):
    barrier = pltpu.get_barrier_semaphore()
    for target in targets:
        pl.semaphore_signal(barrier, inc=1, device_id=target, device_id_type=MESH)
    pl.semaphore_wait(barrier, len(targets))


def paired(me, k, n):
    out, bit = me, 1
    while bit < n:
        if k & bit:
            out = out + bit * (1 - 2 * lax.rem(me // bit, 2))
        bit *= 2
    return out


def tick_kernel(
    n, per, experts, sections,
    x_ref, g_ref, route_ref, len_ref, gain_ref, router_ref, down_ref, up_ref, wg_hbm, wu_hbm, wd_hbm,
    back_out, pd_out, pu_out,
    wg_v, wu_v, wd_v, rows_in, rows_ref, select_ref, stats_ref, lows_ref, stats_in, lows_in,
    gate_acc, up_acc, back_acc, dg_ref, du_ref, ssq, gsum, ssum, vec_ref, dn_ref,
    pdn, pvec, pd_ref, pu_ref, ppd, ppu, sendbuf, landing, result, turn,
    ws, rs, rr, fs, fr, ss, sr, ls, lr, own, qs, qr, ps, pr, es, er, zs, zr,
):
    me = lax.axis_index("expert")
    core = lax.axis_index("dp")
    sec = lax.axis_index("section")
    other = 1 - core
    partner = {"dp": other}
    ahead = {"section": lax.rem(sec + sections - 1, sections)}
    behind = {"section": lax.rem(sec + 1, sections)}
    peers = [paired(me, k, n) for k in range(n)]
    count, width = x_ref.shape
    cap = select_ref.shape[1]
    hidden = wg_v.shape[2]
    f32, bf16 = jnp.float32, jnp.bfloat16

    def weights(k):
        cols = pl.ds(pl.multiple_of(peers[k] * width, LANES), width)
        return [
            pltpu.make_async_copy(wg_hbm.at[0, cols, :], wg_v.at[k], ws.at[k, 0]),
            pltpu.make_async_copy(wu_hbm.at[0, cols, :], wu_v.at[k], ws.at[k, 1]),
            pltpu.make_async_copy(wd_hbm.at[0, :, cols], wd_v.at[k], ws.at[k, 2]),
        ]

    loads = [weights(k) for k in range(n)]
    for k in range(min(DEPTH, n)):
        for copy in loads[k]:
            copy.start()

    def send(src, dst, a, b, k, target):
        copy = pltpu.make_async_remote_copy(
            src_ref=src, dst_ref=dst, send_sem=a.at[k], recv_sem=b.at[k],
            device_id=target, device_id_type=MESH,
        )
        copy.start()
        return copy

    line = lax.broadcasted_iota(jnp.int32, (8, count), 0)
    first = (route_ref[0:1, :] == line).astype(f32)
    second = (route_ref[1:2, :] == line).astype(f32)
    member = first + second
    before = (
        lax.broadcasted_iota(jnp.int32, (count, count), 0)
        < lax.broadcasted_iota(jnp.int32, (count, count), 1)
    ).astype(bf16)
    rank = jnp.dot(member.astype(bf16), before, preferred_element_type=f32)
    place = jnp.where(member > 0, rank, -1.0)
    slot = lax.broadcasted_iota(jnp.int32, (cap, count), 0).astype(f32)
    x, g = x_ref[...], g_ref[...]
    for e in range(experts):
        chosen = (place[e:e + 1, :] == slot).astype(bf16)
        select_ref[e] = chosen
        rows_ref[e, :, :width] = jnp.dot(chosen, x, preferred_element_type=f32).astype(bf16)
        rows_ref[e, :, width:] = jnp.dot(chosen, g, preferred_element_type=f32).astype(bf16)

    greet([{"expert": peer} for peer in peers[1:]] + [partner, ahead, behind])
    mine = pl.ds(pl.multiple_of(core * cap, 16), cap)
    home = rows_ref.at[me // per]
    forwards = [send(home, rows_in.at[0, mine], fs, fr, 0, partner)]
    rows = [
        send(rows_ref.at[peers[k] // per], rows_in.at[k, mine], rs, rr, k - 1, {"expert": peers[k]})
        for k in range(1, n)
    ]
    kept = pltpu.make_async_copy(home, rows_in.at[0, mine], own.at[0])
    kept.start()

    xf = x.astype(f32)
    features = pl.ds(pl.multiple_of(me * width, LANES), width)
    gained = (xf * gain_ref[:, features]).astype(bf16)
    router = jnp.concatenate(
        [router_ref[:, features].astype(f32), jnp.zeros((8 - experts, width), f32)], axis=0
    )
    raw = lax.dot_general(router.astype(bf16), gained, LAST, preferred_element_type=f32)
    square = lax.dot_general(
        jnp.ones((8, width), f32), xf * xf, LAST,
        precision=lax.Precision.HIGHEST, preferred_element_type=f32,
    )
    stats_ref[...] = jnp.where(line < experts, raw, square)
    lows_ref[...] = jnp.concatenate(
        [
            lax.dot_general(gained, down_ref[...], LAST, preferred_element_type=f32),
            lax.dot_general(g, up_ref[...], LAST, preferred_element_type=f32),
        ],
        axis=1,
    ).astype(bf16)
    small = []
    for k in range(1, n):
        target = {"expert": peers[k]}
        small.append(send(stats_ref, stats_in.at[k - 1], ss, sr, k - 1, target))
        small.append(send(lows_ref, lows_in.at[k - 1], ls, lr, k - 1, target))

    def pass_on(k):
        rows[k - 1].wait_recv()
        landed = rows_in.at[k, mine]
        forwards.append(send(landed, landed, fs, fr, k, partner))

    tile = next(t for t in TILES if hidden % t == 0)
    act_tile = next(t for t in (512, 256, 128) if hidden % t == 0)
    kept.wait()
    for k in range(n):
        if k == 1:
            for q in range(1, min(3, n)):
                pass_on(q)
        forwards[k].wait()
        features = pl.ds(pl.multiple_of(peers[k] * width, LANES), width)
        xk = rows_in[k, :, :width].astype(f32)
        part = jnp.sum(xk * xk, axis=1, keepdims=True)
        if k == 0:
            ssq[...] = jnp.broadcast_to(part, ssq.shape)
        else:
            ssq[...] += part
        xk = (xk * gain_ref[:, features]).astype(bf16)
        gk = rows_in[k, :, width:]
        loads[k][0].wait()
        if k + DEPTH < n:
            for copy in loads[k + DEPTH]:
                copy.start()
        if k < n - 1:
            for acc, w, load in ((gate_acc, wg_v, None), (up_acc, wu_v, 1), (back_acc, wd_v, 2)):
                if load is not None:
                    loads[k][load].wait()
                if load == 2 and 3 <= k + 1:
                    pass_on(k + 1)
                for t in range(hidden // tile):
                    c = slice(t * tile, (t + 1) * tile)
                    if load == 2:
                        p = lax.dot_general(gk, w[k, c, :], LAST, preferred_element_type=f32)
                    else:
                        p = jnp.dot(xk, w[k, :, c], preferred_element_type=f32)
                    if k == 0:
                        acc[:, c] = p
                    else:
                        acc[:, c] += p
        else:
            loads[k][1].wait()
            loads[k][2].wait()
            scale = lax.rsqrt(ssq[:, 0:1] / (n * width) + EPS)
            gsum[...] = jnp.zeros_like(gsum)
            ssum[...] = jnp.zeros_like(ssum)
            for t in range(hidden // act_tile):
                c = slice(t * act_tile, (t + 1) * act_tile)
                gate = jnp.dot(xk, wg_v[k, :, c], preferred_element_type=f32)
                up = jnp.dot(xk, wu_v[k, :, c], preferred_element_type=f32)
                back = lax.dot_general(gk, wd_v[k, c, :], LAST, preferred_element_type=f32)
                gate = (gate + gate_acc[:, c]) * scale
                up = (up + up_acc[:, c]) * scale
                back = back + back_acc[:, c]
                sig = jax.nn.sigmoid(gate)
                act = gate * sig
                d_up = back * act
                d_gate = back * up * sig * (1.0 + gate * (1.0 - sig))
                dg_ref[:, c] = d_gate.astype(bf16)
                du_ref[:, c] = d_up.astype(bf16)
                p = d_up * up
                q = d_gate * gate + p
                for j in range(act_tile // LANES):
                    l = slice(j * LANES, (j + 1) * LANES)
                    gsum[...] += p[:, l]
                    ssum[...] += q[:, l]
    lane = lax.broadcasted_iota(jnp.int32, gsum.shape, 1)
    vec_ref[...] = jnp.where(
        lane % 2 == 0,
        jnp.sum(gsum[...], axis=1, keepdims=True),
        jnp.sum(ssum[...], axis=1, keepdims=True),
    )
    theirs = pl.ds(pl.multiple_of(other * cap, 8), cap)
    ours = pl.ds(pl.multiple_of(core * cap, 8), cap)
    shared = [send(vec_ref.at[theirs], pvec, qs, qr, 0, partner)]

    sub = next(t for t in (256, 128) if width % t == 0)
    order = list(range(n - 1, -1, -1))
    blocks, sent, box = {}, {}, {}

    def finish(k):
        blocks[k].wait()
        if not box:
            shared[0].wait()
            v = vec_ref[ours, :] + pvec[...]
            high = v.astype(bf16)
            rest = (v - high.astype(f32)).astype(bf16)
            lane = lax.broadcasted_iota(jnp.int32, v.shape, 1)
            box["packed"] = jnp.where(lane < 2, high.astype(f32), rest.astype(f32)).astype(bf16)
            sendbuf[0, :, width:] = box["packed"]
        sendbuf[k, :, :width] = (dn_ref[k, ours, :] + pdn[k]).astype(bf16)
        if k:
            sendbuf[k, :, width:] = sendbuf[0, :, width:]
            sent[k] = send(
                sendbuf.at[k], landing.at[k - 1], es, er, k - 1, {"expert": peers[k]}
            )

    for i, k in enumerate(order):
        for j in range(width // sub):
            c = slice(j * sub, (j + 1) * sub)
            dn_ref[k, :, c] = lax.dot_general(
                dg_ref[...], wg_v[k, c, :], LAST, preferred_element_type=f32
            ) + lax.dot_general(du_ref[...], wu_v[k, c, :], LAST, preferred_element_type=f32)
            if j == 0 and i > 0:
                finish(order[i - 1])
        blocks[k] = send(dn_ref.at[k, theirs], pdn.at[k], ps, pr, k, partner)

    for copy in small:
        copy.wait()
    stat_rows, low_all = stats_ref[...], lows_ref[...].astype(f32)
    for k in range(1, n):
        stat_rows = stat_rows + stats_in[k - 1]
        low_all = low_all + lows_in[k - 1].astype(f32)
    scale_row = lax.rsqrt(stat_rows[experts:experts + 1, :] / (n * width) + EPS)
    sign_rows = first - second
    spread_row = jnp.sum(
        jnp.where(line < experts, sign_rows * stat_rows, 0.0), axis=0, keepdims=True
    )
    upper = jax.nn.sigmoid(spread_row * scale_row)
    turn[...] = jnp.zeros_like(turn)
    turn[0:8, :] = upper * first + (1.0 - upper) * second
    turn[8:16, :] = sign_rows
    turn[16:17, :] = upper * (1.0 - upper)
    turn[17:18, :] = scale_row
    turn[18:19, :] = spread_row
    token = turn[...].T
    column = lambda i: token[:, i:i + 1]
    delta_of, scale, raw_spread = column(16), column(17), column(18)
    x = x_ref[...].astype(f32)
    ranks = down_ref.shape[0]
    raw_low, g_low = low_all[:, :ranks], low_all[:, ranks:]
    jobs = len_ref.shape[1]
    position = core * count + lax.broadcasted_iota(jnp.int32, (count, ranks), 0)
    owner = jnp.zeros((count, ranks), jnp.int32)
    end = jnp.zeros((1, 1), jnp.int32)
    for j in range(jobs):
        end = end + len_ref[0:1, j:j + 1]
        owner = owner + (end <= position).astype(jnp.int32)
    mask = (
        owner == lax.broadcasted_iota(jnp.int32, (count, ranks), 1) // (ranks // jobs)
    ).astype(f32)
    low = (raw_low * scale * mask).astype(bf16)
    d_low = (ADAPTER_SCALE * g_low * mask).astype(bf16)
    gain = gain_ref[:, pl.ds(pl.multiple_of(me * width, LANES), width)]
    normed = (x * scale * gain).astype(bf16)
    pd_ref[...] = lax.dot_general(d_low, normed, FIRST, preferred_element_type=f32)
    pu_ref[...] = ADAPTER_SCALE * lax.dot_general(low, g_ref[...], FIRST, preferred_element_type=f32)
    shared.append(send(pd_ref, ppd, qs, qr, 1, partner))
    shared.append(send(pu_ref, ppu, qs, qr, 2, partner))
    low_stat = jnp.sum(d_low.astype(f32) * raw_low, axis=1, keepdims=True)
    spread = jnp.zeros((count, 1), f32)
    stat = jnp.zeros((count, 1), f32)
    total = jnp.dot(d_low, down_ref[...], preferred_element_type=f32)

    def add(k, block, total, spread, stat):
        expert = peers[k] // per
        gate, sign = jnp.zeros((count, 1), f32), jnp.zeros((count, 1), f32)
        for e in range(experts):
            mark = (expert == e).astype(f32)
            gate += mark * column(e)
            sign += mark * column(8 + e)
        picked = lax.dot_general(select_ref[expert], block, FIRST, preferred_element_type=f32)
        tail = picked[:, width:]
        spread = spread + sign * (tail[:, 0:1] + tail[:, 2:3])
        stat = stat + gate * (tail[:, 1:2] + tail[:, 3:4])
        return total + gate * picked[:, :width], spread, stat

    finish(0)
    total, spread, stat = add(0, sendbuf[0], total, spread, stat)
    for k in order[:-1]:
        sent[k].wait()
        total, spread, stat = add(k, landing[k - 1], total, spread, stat)
    delta = spread * delta_of
    router = router_ref[:, pl.ds(pl.multiple_of(me * width, LANES), width)].astype(f32)
    for e in range(experts):
        total = total + (delta * column(8 + e)) * router[e:e + 1, :]
    stat = stat / scale + low_stat + delta * raw_spread
    weighted = total * gain
    out = g_ref[...].astype(f32) + scale * weighted - x * (
        scale * scale * scale * stat / (n * width)
    )
    result[...] = out.astype(bf16)
    handed = send(result, back_out, zs, zr, 0, ahead)
    for k in range(1, n):
        rows[k - 1].wait_send()
    shared[1].wait()
    pd_out[...] = pd_ref[...] + ppd[...]
    shared[2].wait()
    pu_out[...] = pu_ref[...] + ppu[...]
    handed.wait()


def settle_kernel(*refs):
    half = len(refs) // 2
    for src, dst in zip(refs[:half], refs[half:]):
        dst[...] = src[...]


def tick(n, per, shards, sections, x, g, routes, lengths, gains, router, down, up, wg, wu, wd):
    count, width = x.shape
    experts = router.shape[0]
    hidden = wg.shape[2]
    ranks = down.shape[0]
    slots = shards * CAP
    f32, bf16 = jnp.float32, jnp.bfloat16
    vmem = pl.BlockSpec(memory_space=pltpu.VMEM)
    hbm = pl.BlockSpec(memory_space=pl.ANY)
    dma = pltpu.SemaphoreType.DMA
    outs = (
        jax.ShapeDtypeStruct((count, width), bf16),
        jax.ShapeDtypeStruct((ranks, width), f32),
        jax.ShapeDtypeStruct((ranks, width), f32),
    )
    values = pl.pallas_call(
        functools.partial(tick_kernel, n, per, experts, sections),
        out_shape=outs,
        in_specs=[vmem] * 8 + [hbm] * 3,
        out_specs=(vmem,) * 3,
        scratch_shapes=[
            pltpu.VMEM((n, width, hidden), bf16),
            pltpu.VMEM((n, width, hidden), bf16),
            pltpu.VMEM((n, hidden, width), bf16),
            pltpu.VMEM((n, slots, 2 * width), bf16),
            pltpu.VMEM((experts, CAP, 2 * width), bf16),
            pltpu.VMEM((experts, CAP, count), bf16),
            pltpu.VMEM((8, count), f32),
            pltpu.VMEM((count, 2 * ranks), bf16),
            pltpu.VMEM((n - 1, 8, count), f32),
            pltpu.VMEM((n - 1, count, 2 * ranks), bf16),
            pltpu.VMEM((slots, hidden), f32),
            pltpu.VMEM((slots, hidden), f32),
            pltpu.VMEM((slots, hidden), f32),
            pltpu.VMEM((slots, hidden), bf16),
            pltpu.VMEM((slots, hidden), bf16),
            pltpu.VMEM((slots, LANES), f32),
            pltpu.VMEM((slots, LANES), f32),
            pltpu.VMEM((slots, LANES), f32),
            pltpu.VMEM((slots, LANES), f32),
            pltpu.VMEM((n, slots, width), f32),
            pltpu.VMEM((n, CAP, width), f32),
            pltpu.VMEM((CAP, LANES), f32),
            pltpu.VMEM((ranks, width), f32),
            pltpu.VMEM((ranks, width), f32),
            pltpu.VMEM((ranks, width), f32),
            pltpu.VMEM((ranks, width), f32),
            pltpu.VMEM((n, CAP, width + LANES), bf16),
            pltpu.VMEM((n - 1, CAP, width + LANES), bf16),
            pltpu.VMEM((count, width), bf16),
            pltpu.VMEM((LANES, count), f32),
            dma((n, 3)),
            dma((n - 1,)), dma((n - 1,)), dma((n,)), dma((n,)),
            dma((n - 1,)), dma((n - 1,)), dma((n - 1,)), dma((n - 1,)),
            dma((1,)), dma((3,)), dma((3,)), dma((n,)), dma((n,)),
            dma((n - 1,)), dma((n - 1,)), dma((1,)), dma((1,)),
        ],
        compiler_params=pltpu.CompilerParams(
            collective_id=0, has_side_effects=True, vmem_limit_bytes=VMEM_LIMIT
        ),
    )(x, g, routes, lengths, gains, router, down, up, wg, wu, wd)
    return pl.pallas_call(
        settle_kernel, out_shape=outs, in_specs=[vmem] * 3, out_specs=(vmem,) * 3
    )(*values)


def body(
    stash,
    cotangent,
    backward_expert_routes,
    backward_job_lengths,
    layer_norm_gains,
    router,
    expert_gate_weight,
    expert_up_weight,
    expert_down_weight,
    adapter_down_maps,
    adapter_up_maps,
):
    n = lax.axis_size("expert")
    shards = lax.axis_size("dp")
    sections = lax.axis_size("section")
    per = n // router.shape[2]
    handed_back, down_grad, up_grad = tick(
        n, per, shards, sections, stash[0], cotangent[0], backward_expert_routes[0].T,
        backward_job_lengths, layer_norm_gains, router[0].T, adapter_down_maps[0].T,
        adapter_up_maps[0], expert_gate_weight, expert_up_weight, expert_down_weight,
    )
    return (handed_back[None], down_grad.T[None], up_grad[None])


def solution(mesh):
    return jax.shard_map(
        body,
        mesh=mesh,
        in_specs=(
            P("section", "dp", "expert"),
            P("section", "dp", "expert"),
            P("section", "dp", None),
            P("section", None),
            P("section", None),
            P("section", None, None),
            P("section", None, ("expert", "dp")),
            P("section", None, ("expert", "dp")),
            P("section", ("expert", "dp"), None),
            P("section", "expert", None),
            P("section", None, "expert"),
        ),
        out_specs=(
            P("section", "dp", "expert"),
            P("section", "expert", None),
            P("section", None, "expert"),
        ),
        check_vma=False,
    )
```

time: 75.2 us -> 49.9 us (0.66)
  Pallas kernels: 61.6 us -> 49.1 us
  local copies, waits for them, and re-layouts: 10.1 us -> 0 us
  other arithmetic: 2.15 us -> 0 us
    pallas_call x3 -> x2, Pallas kernels: 61.6 us -> 49.1 us  [the longest x1 47.3 us: tick(): pl.pallas_call(functools.partial(tick_kernel, n, per, experts, sections),...]
    unnamed x10 -> x0, local copies, waits for them, and re-layouts: 6.47 us -> none
    convert_element_type x2 -> x0, other arithmetic: 1.38 us -> none  [the longest x1 0.71 us: job_columns(): return (owner[:, None] == column_owner[None, :]).astype(jnp.float32)]
    dynamic_slice x1 -> x0, local copies, waits for them, and re-layouts: 1.27 us -> none  [body(): gain = lax.dynamic_slice_in_dim(layer_norm_gains, me * width, width, 1)]
    concatenate x1 -> x0, local copies, waits for them, and re-layouts: 0.77 us -> none  [body(): jnp.concatenate(columns + [jnp.zeros((count, -used % LANES), jnp.float32)...]
    eq x1 -> x0, local copies, waits for them, and re-layouts: 0.76 us -> none  [body(): first = (routes[:, 0:1] == labels[None, :]).astype(jnp.float32)]
where the time goes in v1:
time: 49.9 us; the launch traced here: 49.7 us
  Pallas kernels  49.1 us (98%)
  between operations  0.64 us (1%)
    pallas_call x1, Pallas kernels, tick(): pl.pallas_call(functools.partial(tick_kernel, n, per, experts, sections),...  47.3 us
    pallas_call x1, Pallas kernels, tick(): pl.pallas_call(settle_kernel, out_shape=outs, in_specs=[vmem] * 3, out_sp...  1.78 us

profile of v1, /device:TPU:0, one launch (start us, length us, event | category | flops | bytes accessed | tf_op | source)
XLA Modules:
  0.0 49.7 jit_solution(5832944037088493972)
XLA Ops:
  0.6 47.3 %shard_map.130 = (bf16[128,512]{1,0:T(8,128)(2,1)}, f32[64,512]{1,0:T(8,128)}, f32[64,512]{1,0:T(8,128)}) custom-call(bf16[128,512]{1,0:T(8,128)(2,1)} %bitcast.17, bf16[128,512]{1,0:T(8,128)(2,1)} %bitcast.18, s32[2,128]{1,0:T(2,128)} %bitcast.22, s32[1,4]{1,0:T(1,128)} %len_ref.1, f32[1,2048]{1,0:T(1,128)} %gain_ref.1, bf16[4,2048]{1,0:T(4,128)(2,1)} %bitcast.21, ...), custom_call_target="tpu_custom_call" | custom-call | tf_op jit(solution)/shard_map/pallas_call | solution.py:351
  48.0 1.8 %shard_map.131 = (bf16[128,512]{1,0:T(8,128)(2,1)}, f32[64,512]{1,0:T(8,128)}, f32[64,512]{1,0:T(8,128)}) custom-call(bf16[128,512]{1,0:T(8,128)(2,1)} %get-tuple-element.9.refs_0_, f32[64,512]{1,0:T(8,128)} %get-tuple-element.10.refs_1_, f32[64,512]{1,0:T(8,128)} %get-tuple-element.11.refs_2_), custom_call_target="tpu_custom_call" | custom-call | tf_op jit(solution)/shard_map/pallas_call | solution.py:397

commit v2 on v1

v2 whole, which is shorter than its diff:
```python
import functools

import jax
import jax.numpy as jnp
from jax import lax
from jax.experimental import pallas as pl
from jax.experimental.pallas import tpu as pltpu
from jax.sharding import PartitionSpec as P

CAP = 80

EPS = 1e-05
ADAPTER_SCALE = 0.5
MESH = pl.DeviceIdType.MESH
VMEM_LIMIT = 63 * 1024 * 1024
LANES = 128
DEPTH = 6
TILES = (1792, 896, 512, 256, 128)
ACT_TILES = (512, 256, 128)
LAST = (((1,), (1,)), ((), ()))
FIRST = (((0,), (0,)), ((), ()))


def paired(me, k, n):
    out, bit = me, 1
    while bit < n:
        if k & bit:
            out = out + bit * (1 - 2 * lax.rem(me // bit, 2))
        bit *= 2
    return out


def tick_kernel(
    n, per, experts, sections,
    x_ref, g_ref, route_ref, len_ref, gain_ref, router_ref, down_ref, up_ref, wg_hbm, wu_hbm, wd_hbm,
    back_out, pd_out, pu_out,
    wg_v, wu_v, wd_v, xs_in, gs_in, xs_ref, gs_ref, select_ref, stats_ref, lows_ref, stats_in, lows_in,
    gate_acc, up_acc, back_acc, dg_ref, du_ref, ssq, gsum, ssum, vec_ref, dn_ref,
    pdn, pvec, vsend, vec_in, pd_ref, pu_ref, ppd, ppu, sendbuf, landing, out_ref, result, turn,
    ws, xs_s, xs_r, gs_s, gs_r, xfs, xfr, gfs, gfr, ss, sr, ls, lr, own, qs, qr, vs, vr, ps, pr,
    es, er, zs, zr,
):
    me = lax.axis_index("expert")
    core = lax.axis_index("dp")
    sec = lax.axis_index("section")
    other = 1 - core
    partner = {"dp": other}
    ahead = {"section": lax.rem(sec + sections - 1, sections)}
    behind = {"section": lax.rem(sec + 1, sections)}
    peers = [paired(me, k, n) for k in range(n)]
    count, width = x_ref.shape
    cap = select_ref.shape[1]
    hidden = wg_v.shape[2]
    f32, bf16 = jnp.float32, jnp.bfloat16

    def weights(k):
        cols = pl.ds(pl.multiple_of(peers[k] * width, LANES), width)
        return [
            pltpu.make_async_copy(wg_hbm.at[0, cols, :], wg_v.at[k], ws.at[k, 0]),
            pltpu.make_async_copy(wu_hbm.at[0, cols, :], wu_v.at[k], ws.at[k, 1]),
            pltpu.make_async_copy(wd_hbm.at[0, :, cols], wd_v.at[k], ws.at[k, 2]),
        ]

    inner = list(range(1, n - 1))
    groups = [inner[i:i + 2] for i in range(0, len(inner), 2)] + [[n - 1]]
    blocks_of = [weights(k) for k in range(n)]
    loads = list(blocks_of[0])
    for group in groups:
        loads += [blocks_of[k][i] for k in group for i in (0, 1)] + [blocks_of[k][2] for k in group]
    for copy in loads[:DEPTH]:
        copy.start()
    loaded = [0]

    def load(count):
        for _ in range(count):
            loads[loaded[0]].wait()
            if loaded[0] + DEPTH < len(loads):
                loads[loaded[0] + DEPTH].start()
            loaded[0] += 1

    neighbours = [{"expert": peer} for peer in peers[1:]] + [partner, ahead, behind]
    barrier = pltpu.get_barrier_semaphore()
    for target in neighbours:
        pl.semaphore_signal(barrier, inc=1, device_id=target, device_id_type=MESH)

    def send(src, dst, a, b, k, target):
        copy = pltpu.make_async_remote_copy(
            src_ref=src, dst_ref=dst, send_sem=a.at[k], recv_sem=b.at[k],
            device_id=target, device_id_type=MESH,
        )
        copy.start()
        return copy

    line = lax.broadcasted_iota(jnp.int32, (8, count), 0)
    first = (route_ref[0:1, :] == line).astype(f32)
    second = (route_ref[1:2, :] == line).astype(f32)
    member = first + second
    before = (
        lax.broadcasted_iota(jnp.int32, (count, count), 0)
        < lax.broadcasted_iota(jnp.int32, (count, count), 1)
    ).astype(bf16)
    rank = jnp.dot(member.astype(bf16), before, preferred_element_type=f32)
    place = jnp.where(member > 0, rank, -1.0)
    slot = lax.broadcasted_iota(jnp.int32, (cap, count), 0).astype(f32)
    x, g = x_ref[...], g_ref[...]
    for e in range(experts):
        chosen = (place[e:e + 1, :] == slot).astype(bf16)
        select_ref[e] = chosen
        xs_ref[e] = jnp.dot(chosen, x, preferred_element_type=f32).astype(bf16)
        gs_ref[e] = jnp.dot(chosen, g, preferred_element_type=f32).astype(bf16)

    pl.semaphore_wait(barrier, len(neighbours))
    mine = pl.ds(pl.multiple_of(core * cap, 16), cap)
    home = me // per
    xs_on = [send(xs_ref.at[home], xs_in.at[0, mine], xfs, xfr, 0, partner)]
    gs_on = [send(gs_ref.at[home], gs_in.at[0, mine], gfs, gfr, 0, partner)]
    xs, gs = {}, {}
    for group in groups:
        for k in group:
            xs[k] = send(
                xs_ref.at[peers[k] // per], xs_in.at[k, mine], xs_s, xs_r, k - 1, {"expert": peers[k]}
            )
        for k in group:
            gs[k] = send(
                gs_ref.at[peers[k] // per], gs_in.at[k, mine], gs_s, gs_r, k - 1, {"expert": peers[k]}
            )
    kept = [
        pltpu.make_async_copy(xs_ref.at[home], xs_in.at[0, mine], own.at[0]),
        pltpu.make_async_copy(gs_ref.at[home], gs_in.at[0, mine], own.at[1]),
    ]
    for copy in kept:
        copy.start()

    xf = x.astype(f32)
    features = pl.ds(pl.multiple_of(me * width, LANES), width)
    gained = (xf * gain_ref[:, features]).astype(bf16)
    router = jnp.concatenate(
        [router_ref[:, features].astype(f32), jnp.zeros((8 - experts, width), f32)], axis=0
    )
    raw = lax.dot_general(router.astype(bf16), gained, LAST, preferred_element_type=f32)
    square = lax.dot_general(
        jnp.ones((8, width), f32), xf * xf, LAST,
        precision=lax.Precision.HIGHEST, preferred_element_type=f32,
    )
    stats_ref[...] = jnp.where(line < experts, raw, square)
    lows_ref[...] = jnp.concatenate(
        [
            lax.dot_general(gained, down_ref[...], LAST, preferred_element_type=f32),
            lax.dot_general(g, up_ref[...], LAST, preferred_element_type=f32),
        ],
        axis=1,
    ).astype(bf16)
    small = []
    for k in range(1, n):
        target = {"expert": peers[k]}
        small.append(send(stats_ref, stats_in.at[k - 1], ss, sr, k - 1, target))
        small.append(send(lows_ref, lows_in.at[k - 1], ls, lr, k - 1, target))

    def pass_on(group, arrived, buffer, onward, a, b):
        for k in group:
            arrived[k].wait_recv()
            landed = buffer.at[k, mine]
            onward.append(send(landed, landed, a, b, k, partner))

    pass_x = lambda group: pass_on(group, xs, xs_in, xs_on, xfs, xfr)
    pass_g = lambda group: pass_on(group, gs, gs_in, gs_on, gfs, gfr)

    tile = next(t for t in TILES if hidden % t == 0)

    def add_to(acc, k, c, p):
        if k == 0:
            acc[:, c] = p
        else:
            acc[:, c] += p

    def scaled(k):
        xs_on[k].wait()
        xk = xs_in[k].astype(f32)
        part = jnp.sum(xk * xk, axis=1, keepdims=True)
        if k == 0:
            ssq[...] = jnp.broadcast_to(part, ssq.shape)
        else:
            ssq[...] += part
        features = pl.ds(pl.multiple_of(peers[k] * width, LANES), width)
        return (xk * gain_ref[:, features]).astype(bf16)

    def forth(k):
        load(2)
        xk = scaled(k)
        for t in range(hidden // tile):
            c = slice(t * tile, (t + 1) * tile)
            add_to(gate_acc, k, c, jnp.dot(xk, wg_v[k, :, c], preferred_element_type=f32))
            add_to(up_acc, k, c, jnp.dot(xk, wu_v[k, :, c], preferred_element_type=f32))

    def back_from(k):
        load(1)
        gs_on[k].wait()
        for t in range(hidden // tile):
            c = slice(t * tile, (t + 1) * tile)
            add_to(back_acc, k, c, lax.dot_general(
                gs_in[k], wd_v[k, c, :], LAST, preferred_element_type=f32
            ))

    for copy in kept:
        copy.wait()
    forth(0)
    back_from(0)
    pass_x(groups[0])
    for i, group in enumerate(groups[:-1]):
        for j, k in enumerate(group):
            forth(k)
            if j == 0:
                pass_g(group)
        pass_x(groups[i + 1])
        for k in group:
            back_from(k)
    k = n - 1
    pass_g(groups[-1])
    load(2)
    xk = scaled(k)
    load(1)
    gs_on[k].wait()
    scale = lax.rsqrt(ssq[:, 0:1] / (n * width) + EPS)
    gk = gs_in[k]
    gate_sum = jnp.zeros(gsum.shape, f32)
    stat_sum = jnp.zeros(gsum.shape, f32)
    act_tile = next(t for t in ACT_TILES if hidden % t == 0)
    for t in range(hidden // act_tile):
        c = slice(t * act_tile, (t + 1) * act_tile)
        gate = jnp.dot(xk, wg_v[k, :, c], preferred_element_type=f32)
        up = jnp.dot(xk, wu_v[k, :, c], preferred_element_type=f32)
        back = lax.dot_general(gk, wd_v[k, c, :], LAST, preferred_element_type=f32)
        gate = (gate + gate_acc[:, c]) * scale
        up = (up + up_acc[:, c]) * scale
        back = back + back_acc[:, c]
        sig = jax.nn.sigmoid(gate)
        act = gate * sig
        both = back * up
        d_gate = both * (sig + act * (1.0 - sig))
        dg_ref[:, c] = d_gate.astype(bf16)
        du_ref[:, c] = (back * act).astype(bf16)
        p, q = both * act, d_gate * gate
        for j in range(act_tile // LANES):
            l = slice(j * LANES, (j + 1) * LANES)
            gate_sum += p[:, l]
            stat_sum += q[:, l]
    gsum[...] = gate_sum
    ssum[...] = stat_sum
    theirs = pl.ds(pl.multiple_of(other * cap, 8), cap)
    ours = pl.ds(pl.multiple_of(core * cap, 8), cap)

    order = list(range(n - 1, -1, -1))
    shared, halves, sent, told = [], {}, {}, []

    def finish(k):
        halves[k].wait()
        sendbuf[k] = (dn_ref[k, ours, :] + pdn[k]).astype(bf16)
        if k:
            sent[k] = send(sendbuf.at[k], landing.at[k - 1], es, er, k - 1, {"expert": peers[k]})

    def tell():
        shared[0].wait()
        v = vec_ref[ours, :] + pvec[...]
        high = v.astype(bf16)
        rest = (v - high.astype(f32)).astype(bf16)
        lane = lax.broadcasted_iota(jnp.int32, v.shape, 1)
        vsend[...] = jnp.where(lane < 2, high.astype(f32), rest.astype(f32)).astype(bf16)
        for k in range(1, n):
            told.append(send(vsend, vec_in.at[k - 1], vs, vr, k - 1, {"expert": peers[k]}))

    sub = next(t for t in (256, 128) if width % t == 0)

    def gradient(k, d_ref, w_ref, fresh):
        for j in range(width // sub):
            c = slice(j * sub, (j + 1) * sub)
            p = lax.dot_general(d_ref[...], w_ref[k, c, :], LAST, preferred_element_type=f32)
            if fresh:
                dn_ref[k, :, c] = p
            else:
                dn_ref[k, :, c] += p

    for i, k in enumerate(order):
        if k:
            for j in range(width // sub):
                c = slice(j * sub, (j + 1) * sub)
                dn_ref[k, :, c] = lax.dot_general(
                    dg_ref[...], wg_v[k, c, :], LAST, preferred_element_type=f32
                ) + lax.dot_general(du_ref[...], wu_v[k, c, :], LAST, preferred_element_type=f32)
        else:
            gradient(k, dg_ref, wg_v, True)
            finish(order[i - 1])
            gradient(k, du_ref, wu_v, False)
        if i == 0:
            gate_sum, stat_sum = gsum[...], ssum[...]
            total = jnp.sum(gate_sum, axis=1, keepdims=True)
            lane = lax.broadcasted_iota(jnp.int32, gsum.shape, 1)
            vec_ref[...] = jnp.where(
                lane % 2 == 0, total, total + jnp.sum(stat_sum, axis=1, keepdims=True)
            )
            shared.append(send(vec_ref.at[theirs], pvec, qs, qr, 0, partner))
        halves[k] = send(dn_ref.at[k, theirs], pdn.at[k], ps, pr, k, partner)
        if i == 1:
            tell()
        if 0 < i and k:
            finish(order[i - 1])

    for copy in small:
        copy.wait()
    stat_rows, low_all = stats_ref[...], lows_ref[...].astype(f32)
    for k in range(1, n):
        stat_rows = stat_rows + stats_in[k - 1]
        low_all = low_all + lows_in[k - 1].astype(f32)
    scale_row = lax.rsqrt(stat_rows[experts:experts + 1, :] / (n * width) + EPS)
    sign_rows = first - second
    spread_row = jnp.sum(
        jnp.where(line < experts, sign_rows * stat_rows, 0.0), axis=0, keepdims=True
    )
    upper = jax.nn.sigmoid(spread_row * scale_row)
    turn[...] = jnp.zeros_like(turn)
    turn[0:8, :] = upper * first + (1.0 - upper) * second
    turn[8:16, :] = sign_rows
    turn[16:17, :] = upper * (1.0 - upper)
    turn[17:18, :] = scale_row
    turn[18:19, :] = spread_row
    token = turn[...].T
    column = lambda i: token[:, i:i + 1]
    delta_of, scale, raw_spread = column(16), column(17), column(18)
    x = x_ref[...].astype(f32)
    ranks = down_ref.shape[0]
    raw_low, g_low = low_all[:, :ranks], low_all[:, ranks:]
    jobs = len_ref.shape[1]
    position = core * count + lax.broadcasted_iota(jnp.int32, (count, ranks), 0)
    owner = jnp.zeros((count, ranks), jnp.int32)
    end = jnp.zeros((1, 1), jnp.int32)
    for j in range(jobs):
        end = end + len_ref[0:1, j:j + 1]
        owner = owner + (end <= position).astype(jnp.int32)
    mask = (
        owner == lax.broadcasted_iota(jnp.int32, (count, ranks), 1) // (ranks // jobs)
    ).astype(f32)
    low = (raw_low * scale * mask).astype(bf16)
    d_low = (ADAPTER_SCALE * g_low * mask).astype(bf16)
    gain = gain_ref[:, pl.ds(pl.multiple_of(me * width, LANES), width)]
    normed = (x * scale * gain).astype(bf16)
    pd_ref[...] = lax.dot_general(d_low, normed, FIRST, preferred_element_type=f32)
    pu_ref[...] = ADAPTER_SCALE * lax.dot_general(low, g_ref[...], FIRST, preferred_element_type=f32)
    shared.append(send(pd_ref, ppd, qs, qr, 1, partner))
    shared.append(send(pu_ref, ppu, qs, qr, 2, partner))

    def share(k):
        expert = peers[k] // per
        gate, sign = jnp.zeros((count, 1), f32), jnp.zeros((count, 1), f32)
        for e in range(experts):
            mark = (expert == e).astype(f32)
            gate += mark * column(e)
            sign += mark * column(8 + e)
        return select_ref[expert], gate, sign

    spread = jnp.zeros((count, 1), f32)
    stat = jnp.zeros((count, 1), f32)
    for copy in told:
        copy.wait()
    for k in range(n):
        chosen, gate, sign = share(k)
        terms = vsend[...] if k == 0 else vec_in[k - 1]
        picked = lax.dot_general(chosen, terms, FIRST, preferred_element_type=f32)
        spread = spread + sign * (picked[:, 0:1] + picked[:, 2:3])
        stat = stat + gate * (picked[:, 1:2] + picked[:, 3:4])
    delta = spread * delta_of
    low_stat = jnp.sum(d_low.astype(f32) * raw_low, axis=1, keepdims=True)
    stat = stat / scale + low_stat + delta * raw_spread
    total = jnp.dot(d_low, down_ref[...], preferred_element_type=f32)
    router = router_ref[:, pl.ds(pl.multiple_of(me * width, LANES), width)].astype(f32)
    for e in range(experts):
        total = total + (delta * column(8 + e)) * router[e:e + 1, :]
    out_ref[...] = g_ref[...].astype(f32) + scale * (total * gain) - x * (
        scale * scale * scale * stat / (n * width)
    )

    def add(k, block):
        chosen, gate, _ = share(k)
        picked = lax.dot_general(chosen, block, FIRST, preferred_element_type=f32)
        return out_ref[...] + (gate * scale) * gain * picked

    finish(0)
    out_ref[...] = add(0, sendbuf[0])
    for k in order[:-2]:
        sent[k].wait()
        out_ref[...] = add(k, landing[k - 1])
    last = order[-2]
    sent[last].wait_recv()
    result[...] = add(last, landing[last - 1]).astype(bf16)
    handed = send(result, back_out, zs, zr, 0, ahead)
    sent[last].wait_send()
    for k in range(1, n):
        xs[k].wait_send()
        gs[k].wait_send()
    shared[1].wait()
    pd_out[...] = pd_ref[...] + ppd[...]
    shared[2].wait()
    pu_out[...] = pu_ref[...] + ppu[...]
    handed.wait()


def settle_kernel(*refs):
    half = len(refs) // 2
    for src, dst in zip(refs[:half], refs[half:]):
        dst[...] = src[...]


def tick(n, per, shards, sections, x, g, routes, lengths, gains, router, down, up, wg, wu, wd):
    count, width = x.shape
    experts = router.shape[0]
    hidden = wg.shape[2]
    ranks = down.shape[0]
    slots = shards * CAP
    f32, bf16 = jnp.float32, jnp.bfloat16
    vmem = pl.BlockSpec(memory_space=pltpu.VMEM)
    hbm = pl.BlockSpec(memory_space=pl.ANY)
    dma = pltpu.SemaphoreType.DMA
    outs = (
        jax.ShapeDtypeStruct((count, width), bf16),
        jax.ShapeDtypeStruct((ranks, width), f32),
        jax.ShapeDtypeStruct((ranks, width), f32),
    )
    values = pl.pallas_call(
        functools.partial(tick_kernel, n, per, experts, sections),
        out_shape=outs,
        in_specs=[vmem] * 8 + [hbm] * 3,
        out_specs=(vmem,) * 3,
        scratch_shapes=[
            pltpu.VMEM((n, width, hidden), bf16),
            pltpu.VMEM((n, width, hidden), bf16),
            pltpu.VMEM((n, hidden, width), bf16),
            pltpu.VMEM((n, slots, width), bf16),
            pltpu.VMEM((n, slots, width), bf16),
            pltpu.VMEM((experts, CAP, width), bf16),
            pltpu.VMEM((experts, CAP, width), bf16),
            pltpu.VMEM((experts, CAP, count), bf16),
            pltpu.VMEM((8, count), f32),
            pltpu.VMEM((count, 2 * ranks), bf16),
            pltpu.VMEM((n - 1, 8, count), f32),
            pltpu.VMEM((n - 1, count, 2 * ranks), bf16),
            pltpu.VMEM((slots, hidden), f32),
            pltpu.VMEM((slots, hidden), f32),
            pltpu.VMEM((slots, hidden), f32),
            pltpu.VMEM((slots, hidden), bf16),
            pltpu.VMEM((slots, hidden), bf16),
            pltpu.VMEM((slots, LANES), f32),
            pltpu.VMEM((slots, LANES), f32),
            pltpu.VMEM((slots, LANES), f32),
            pltpu.VMEM((slots, LANES), f32),
            pltpu.VMEM((n, slots, width), f32),
            pltpu.VMEM((n, CAP, width), f32),
            pltpu.VMEM((CAP, LANES), f32),
            pltpu.VMEM((CAP, LANES), bf16),
            pltpu.VMEM((n - 1, CAP, LANES), bf16),
            pltpu.VMEM((ranks, width), f32),
            pltpu.VMEM((ranks, width), f32),
            pltpu.VMEM((ranks, width), f32),
            pltpu.VMEM((ranks, width), f32),
            pltpu.VMEM((n, CAP, width), bf16),
            pltpu.VMEM((n - 1, CAP, width), bf16),
            pltpu.VMEM((count, width), f32),
            pltpu.VMEM((count, width), bf16),
            pltpu.VMEM((LANES, count), f32),
            dma((n, 3)),
            *[dma((n - 1,))] * 4, *[dma((n,))] * 4, *[dma((n - 1,))] * 4,
            dma((2,)), dma((3,)), dma((3,)), *[dma((n - 1,))] * 2, *[dma((n,))] * 2,
            *[dma((n - 1,))] * 2, dma((1,)), dma((1,)),
        ],
        compiler_params=pltpu.CompilerParams(
            collective_id=0, has_side_effects=True, vmem_limit_bytes=VMEM_LIMIT
        ),
    )(x, g, routes, lengths, gains, router, down, up, wg, wu, wd)
    return pl.pallas_call(
        settle_kernel, out_shape=outs, in_specs=[vmem] * 3, out_specs=(vmem,) * 3
    )(*values)


def body(
    stash,
    cotangent,
    backward_expert_routes,
    backward_job_lengths,
    layer_norm_gains,
    router,
    expert_gate_weight,
    expert_up_weight,
    expert_down_weight,
    adapter_down_maps,
    adapter_up_maps,
):
    n = lax.axis_size("expert")
    shards = lax.axis_size("dp")
    sections = lax.axis_size("section")
    per = n // router.shape[2]
    handed_back, down_grad, up_grad = tick(
        n, per, shards, sections, stash[0], cotangent[0], backward_expert_routes[0].T,
        backward_job_lengths, layer_norm_gains, router[0].T, adapter_down_maps[0].T,
        adapter_up_maps[0], expert_gate_weight, expert_up_weight, expert_down_weight,
    )
    return (handed_back[None], down_grad.T[None], up_grad[None])


def solution(mesh):
    return jax.shard_map(
        body,
        mesh=mesh,
        in_specs=(
            P("section", "dp", "expert"),
            P("section", "dp", "expert"),
            P("section", "dp", None),
            P("section", None),
            P("section", None),
            P("section", None, None),
            P("section", None, ("expert", "dp")),
            P("section", None, ("expert", "dp")),
            P("section", ("expert", "dp"), None),
            P("section", "expert", None),
            P("section", None, "expert"),
        ),
        out_specs=(
            P("section", "dp", "expert"),
            P("section", "expert", None),
            P("section", None, "expert"),
        ),
        check_vma=False,
    )
```

time: 49.9 us -> 43.1 us (0.86)
  Pallas kernels: 49.1 us -> 42.3 us
    pallas_call x1, Pallas kernels: 47.3 us -> 40.5 us  [tick(): pl.pallas_call(functools.partial(tick_kernel, n, per, experts, sections),...]
where the time goes in v2:
time: 43.1 us; the launch traced here: 43 us
  Pallas kernels  42.3 us (98%)
  between operations  0.64 us (1%)
    pallas_call x1, Pallas kernels, tick(): pl.pallas_call(functools.partial(tick_kernel, n, per, experts, sections),...  40.5 us
    pallas_call x1, Pallas kernels, tick(): pl.pallas_call(settle_kernel, out_shape=outs, in_specs=[vmem] * 3, out_sp...  1.78 us

profile of v2, /device:TPU:0, one launch (start us, length us, event | category | flops | bytes accessed | tf_op | source)
XLA Modules:
  0.0 43.0 jit_solution(17754700951188683461)
XLA Ops:
  0.6 40.5 %shard_map.130 = (bf16[128,512]{1,0:T(8,128)(2,1)}, f32[64,512]{1,0:T(8,128)}, f32[64,512]{1,0:T(8,128)}) custom-call(bf16[128,512]{1,0:T(8,128)(2,1)} %bitcast.17, bf16[128,512]{1,0:T(8,128)(2,1)} %bitcast.18, s32[2,128]{1,0:T(2,128)} %bitcast.22, s32[1,4]{1,0:T(1,128)} %len_ref.1, f32[1,2048]{1,0:T(1,128)} %gain_ref.1, bf16[4,2048]{1,0:T(4,128)(2,1)} %bitcast.21, ...), custom_call_target="tpu_custom_call" | custom-call | tf_op jit(solution)/shard_map/pallas_call | solution.py:426
  41.2 1.8 %shard_map.131 = (bf16[128,512]{1,0:T(8,128)(2,1)}, f32[64,512]{1,0:T(8,128)}, f32[64,512]{1,0:T(8,128)}) custom-call(bf16[128,512]{1,0:T(8,128)(2,1)} %get-tuple-element.9.refs_0_, f32[64,512]{1,0:T(8,128)} %get-tuple-element.10.refs_1_, f32[64,512]{1,0:T(8,128)} %get-tuple-element.11.refs_2_), custom_call_target="tpu_custom_call" | custom-call | tf_op jit(solution)/shard_map/pallas_call | solution.py:476

commit v3 on v2

--- a/solution.py
+++ b/solution.py
@@ -12,7 +12,7 @@
 EPS = 1e-05
 ADAPTER_SCALE = 0.5
 MESH = pl.DeviceIdType.MESH
-VMEM_LIMIT = 63 * 1024 * 1024
+VMEM_LIMIT = 62 * 1024 * 1024
 LANES = 128
 DEPTH = 6
 TILES = (1792, 896, 512, 256, 128)
@@ -35,10 +35,10 @@
     x_ref, g_ref, route_ref, len_ref, gain_ref, router_ref, down_ref, up_ref, wg_hbm, wu_hbm, wd_hbm,
     back_out, pd_out, pu_out,
     wg_v, wu_v, wd_v, xs_in, gs_in, xs_ref, gs_ref, select_ref, stats_ref, lows_ref, stats_in, lows_in,
-    gate_acc, up_acc, back_acc, dg_ref, du_ref, ssq, gsum, ssum, vec_ref, dn_ref,
-    pdn, pvec, vsend, vec_in, pd_ref, pu_ref, ppd, ppu, sendbuf, landing, out_ref, result, turn,
+    gate_acc, up_acc, back_acc, dg_ref, du_ref, ssq, gsum, ssum, vec_ref, dn_ref, dn_own,
+    pdn, pdn_own, pvec, vsend, vec_in, pd_ref, pu_ref, ppd, ppu, sendbuf, landing, out_ref, result, turn,
     ws, xs_s, xs_r, gs_s, gs_r, xfs, xfr, gfs, gfr, ss, sr, ls, lr, own, qs, qr, vs, vr, ps, pr,
-    es, er, zs, zr,
+    es, er, os, ox, zs, zr,
 ):
     me = lax.axis_index("expert")
     core = lax.axis_index("dp")
@@ -249,14 +249,24 @@
     theirs = pl.ds(pl.multiple_of(other * cap, 8), cap)
     ours = pl.ds(pl.multiple_of(core * cap, 8), cap)
 
-    order = list(range(n - 1, -1, -1))
+    sub = next(t for t in (256, 128) if width % t == 0)
+    parts = [slice(j * sub, (j + 1) * sub) for j in range(width // sub)]
+    units = [(k, j) for j in range(len(parts)) for k in range(n - 1, 0, -1)]
+    pairs = [units[i:i + 2] for i in range(0, len(units), 2)]
     shared, halves, sent, told = [], {}, {}, []
 
-    def finish(k):
-        halves[k].wait()
-        sendbuf[k] = (dn_ref[k, ours, :] + pdn[k]).astype(bf16)
-        if k:
-            sent[k] = send(sendbuf.at[k], landing.at[k - 1], es, er, k - 1, {"expert": peers[k]})
+    def exchange(k, j):
+        halves[k, j] = send(
+            dn_ref.at[k, j, theirs], pdn.at[k, j], ps, pr, k * len(parts) + j, partner
+        )
+
+    def finish(k, j):
+        halves[k, j].wait()
+        sendbuf[k, j] = (dn_ref[k, j, ours, :] + pdn[k, j]).astype(bf16)
+        sent[k, j] = send(
+            sendbuf.at[k, j], landing.at[k - 1, j], es, er, (k - 1) * len(parts) + j,
+            {"expert": peers[k]},
+        )
 
     def tell():
         shared[0].wait()
@@ -268,44 +278,26 @@
         for k in range(1, n):
             told.append(send(vsend, vec_in.at[k - 1], vs, vr, k - 1, {"expert": peers[k]}))
 
-    sub = next(t for t in (256, 128) if width % t == 0)
-
-    def gradient(k, d_ref, w_ref, fresh):
-        for j in range(width // sub):
-            c = slice(j * sub, (j + 1) * sub)
-            p = lax.dot_general(d_ref[...], w_ref[k, c, :], LAST, preferred_element_type=f32)
-            if fresh:
-                dn_ref[k, :, c] = p
-            else:
-                dn_ref[k, :, c] += p
-
-    for i, k in enumerate(order):
-        if k:
-            for j in range(width // sub):
-                c = slice(j * sub, (j + 1) * sub)
-                dn_ref[k, :, c] = lax.dot_general(
-                    dg_ref[...], wg_v[k, c, :], LAST, preferred_element_type=f32
-                ) + lax.dot_general(du_ref[...], wu_v[k, c, :], LAST, preferred_element_type=f32)
-        else:
-            gradient(k, dg_ref, wg_v, True)
-            finish(order[i - 1])
-            gradient(k, du_ref, wu_v, False)
-        if i == 0:
-            gate_sum, stat_sum = gsum[...], ssum[...]
-            total = jnp.sum(gate_sum, axis=1, keepdims=True)
-            lane = lax.broadcasted_iota(jnp.int32, gsum.shape, 1)
-            vec_ref[...] = jnp.where(
-                lane % 2 == 0, total, total + jnp.sum(stat_sum, axis=1, keepdims=True)
-            )
-            shared.append(send(vec_ref.at[theirs], pvec, qs, qr, 0, partner))
-        halves[k] = send(dn_ref.at[k, theirs], pdn.at[k], ps, pr, k, partner)
-        if i == 1:
-            tell()
-        if 0 < i and k:
-            finish(order[i - 1])
-
+    def product(d_ref, w_ref, k, j):
+        return lax.dot_general(d_ref[...], w_ref[k, parts[j], :], LAST, preferred_element_type=f32)
+
+    def region(pair):
+        for k, j in pair:
+            dn_ref[k, j] = product(dg_ref, wg_v, k, j) + product(du_ref, wu_v, k, j)
+
+    region(pairs[0])
+    total = jnp.sum(gsum[...], axis=1, keepdims=True)
+    lane = lax.broadcasted_iota(jnp.int32, gsum.shape, 1)
+    vec_ref[...] = jnp.where(
+        lane % 2 == 0, total, total + jnp.sum(ssum[...], axis=1, keepdims=True)
+    )
+    shared.append(send(vec_ref.at[theirs], pvec, qs, qr, 0, partner))
+    for unit in pairs[0]:
+        exchange(*unit)
     for copy in small:
         copy.wait()
+    for pair in pairs[1:2]:
+        region(pair)
     stat_rows, low_all = stats_ref[...], lows_ref[...].astype(f32)
     for k in range(1, n):
         stat_rows = stat_rows + stats_in[k - 1]
@@ -344,9 +336,36 @@
     normed = (x * scale * gain).astype(bf16)
     pd_ref[...] = lax.dot_general(d_low, normed, FIRST, preferred_element_type=f32)
     pu_ref[...] = ADAPTER_SCALE * lax.dot_general(low, g_ref[...], FIRST, preferred_element_type=f32)
-    shared.append(send(pd_ref, ppd, qs, qr, 1, partner))
-    shared.append(send(pu_ref, ppu, qs, qr, 2, partner))
-
+    for i, pair in enumerate(pairs[1:]):
+        if i:
+            region(pair)
+        for unit in pair:
+            exchange(*unit)
+        if i == 0:
+            tell()
+            shared.append(send(pd_ref, ppd, qs, qr, 1, partner))
+            shared.append(send(pu_ref, ppu, qs, qr, 2, partner))
+        for unit in pairs[i]:
+            finish(*unit)
+    for copy in told:
+        copy.wait()
+
+    def own_region(j):
+        dn_ref[0, j] = product(dg_ref, wg_v, 0, j)
+        dn_own[j] = product(du_ref, wu_v, 0, j)
+
+    def own_exchange(j):
+        exchange(0, j)
+        halves[-1, j] = send(dn_own.at[j, theirs], pdn_own.at[j], os, ox, j, partner)
+
+    def own_finish(j):
+        halves[0, j].wait()
+        halves[-1, j].wait()
+        sendbuf[0, j] = (
+            (dn_ref[0, j, ours, :] + dn_own[j, ours, :]) + (pdn[0, j] + pdn_own[j])
+        ).astype(bf16)
+
+    own_region(0)
     def share(k):
         expert = peers[k] // per
         gate, sign = jnp.zeros((count, 1), f32), jnp.zeros((count, 1), f32)
@@ -356,12 +375,12 @@
             sign += mark * column(8 + e)
         return select_ref[expert], gate, sign
 
+    gates = {}
     spread = jnp.zeros((count, 1), f32)
     stat = jnp.zeros((count, 1), f32)
-    for copy in told:
-        copy.wait()
     for k in range(n):
         chosen, gate, sign = share(k)
+        gates[k] = gate * scale
         terms = vsend[...] if k == 0 else vec_in[k - 1]
         picked = lax.dot_general(chosen, terms, FIRST, preferred_element_type=f32)
         spread = spread + sign * (picked[:, 0:1] + picked[:, 2:3])
@@ -377,21 +396,29 @@
         scale * scale * scale * stat / (n * width)
     )
 
-    def add(k, block):
-        chosen, gate, _ = share(k)
-        picked = lax.dot_general(chosen, block, FIRST, preferred_element_type=f32)
-        return out_ref[...] + (gate * scale) * gain * picked
-
-    finish(0)
-    out_ref[...] = add(0, sendbuf[0])
-    for k in order[:-2]:
-        sent[k].wait()
-        out_ref[...] = add(k, landing[k - 1])
-    last = order[-2]
-    sent[last].wait_recv()
-    result[...] = add(last, landing[last - 1]).astype(bf16)
-    handed = send(result, back_out, zs, zr, 0, ahead)
-    sent[last].wait_send()
+
+    own_exchange(0)
+    for unit in pairs[-1]:
+        finish(*unit)
+    for j in range(1, len(parts)):
+        own_region(j)
+        own_exchange(j)
+    handed = []
+    for j, c in enumerate(parts):
+        own_finish(j)
+        for k in range(n - 1, 0, -1):
+            sent[k, j].wait_recv()
+        out = out_ref[:, c]
+        for k in range(n):
+            block = landing[k - 1, j] if k else sendbuf[0, j]
+            picked = lax.dot_general(
+                select_ref[peers[k] // per], block, FIRST, preferred_element_type=f32
+            )
+            out = out + gates[k] * gain[:, c] * picked
+        result[j] = out.astype(bf16)
+        handed.append(send(result.at[j], back_out.at[:, c], zs, zr, j, ahead))
+    for copy in sent.values():
+        copy.wait_send()
     for k in range(1, n):
         xs[k].wait_send()
         gs[k].wait_send()
@@ -399,7 +426,8 @@
     pd_out[...] = pd_ref[...] + ppd[...]
     shared[2].wait()
     pu_out[...] = pu_ref[...] + ppu[...]
-    handed.wait()
+    for copy in handed:
+        copy.wait()
 
 
 def settle_kernel(*refs):
@@ -414,6 +442,8 @@
     hidden = wg.shape[2]
     ranks = down.shape[0]
     slots = shards * CAP
+    sub = next(t for t in (256, 128) if width % t == 0)
+    parts = width // sub
     f32, bf16 = jnp.float32, jnp.bfloat16
     vmem = pl.BlockSpec(memory_space=pltpu.VMEM)
     hbm = pl.BlockSpec(memory_space=pl.ANY)
@@ -425,7 +455,7 @@
     )
     values = pl.pallas_call(
         functools.partial(tick_kernel, n, per, experts, sections),
-        out_shape=outs,
+        out_shape=tuple(pltpu.VMEM(o.shape, o.dtype) for o in outs),
         in_specs=[vmem] * 8 + [hbm] * 3,
         out_specs=(vmem,) * 3,
         scratch_shapes=[
@@ -450,8 +480,10 @@
             pltpu.VMEM((slots, LANES), f32),
             pltpu.VMEM((slots, LANES), f32),
             pltpu.VMEM((slots, LANES), f32),
-            pltpu.VMEM((n, slots, width), f32),
-            pltpu.VMEM((n, CAP, width), f32),
+            pltpu.VMEM((n, parts, slots, sub), f32),
+            pltpu.VMEM((parts, slots, sub), f32),
+            pltpu.VMEM((n, parts, CAP, sub), f32),
+            pltpu.VMEM((parts, CAP, sub), f32),
             pltpu.VMEM((CAP, LANES), f32),
             pltpu.VMEM((CAP, LANES), bf16),
             pltpu.VMEM((n - 1, CAP, LANES), bf16),
@@ -459,15 +491,15 @@
             pltpu.VMEM((ranks, width), f32),
             pltpu.VMEM((ranks, width), f32),
             pltpu.VMEM((ranks, width), f32),
-            pltpu.VMEM((n, CAP, width), bf16),
-            pltpu.VMEM((n - 1, CAP, width), bf16),
+            pltpu.VMEM((n, parts, CAP, sub), bf16),
+            pltpu.VMEM((n - 1, parts, CAP, sub), bf16),
             pltpu.VMEM((count, width), f32),
-            pltpu.VMEM((count, width), bf16),
+            pltpu.VMEM((parts, count, sub), bf16),
             pltpu.VMEM((LANES, count), f32),
             dma((n, 3)),
             *[dma((n - 1,))] * 4, *[dma((n,))] * 4, *[dma((n - 1,))] * 4,
-            dma((2,)), dma((3,)), dma((3,)), *[dma((n - 1,))] * 2, *[dma((n,))] * 2,
-            *[dma((n - 1,))] * 2, dma((1,)), dma((1,)),
+            dma((2,)), dma((3,)), dma((3,)), *[dma((n - 1,))] * 2, *[dma((n * parts,))] * 2,
+            *[dma(((n - 1) * parts,))] * 2, *[dma((parts,))] * 4,
         ],
         compiler_params=pltpu.CompilerParams(
             collective_id=0, has_side_effects=True, vmem_limit_bytes=VMEM_LIMIT
@@ -475,7 +507,7 @@
     )(x, g, routes, lengths, gains, router, down, up, wg, wu, wd)
     return pl.pallas_call(
         settle_kernel, out_shape=outs, in_specs=[vmem] * 3, out_specs=(vmem,) * 3
-    )(*values)
+    )(*[pltpu.with_memory_space_constraint(v, pltpu.VMEM) for v in values])
 
 
 def body(

time: 43.1 us -> 41.6 us (0.965)
  Pallas kernels: 42.3 us -> 40.8 us
    pallas_call x1, Pallas kernels: 1.78 us -> 0.77 us  [tick(): pl.pallas_call(settle_kernel, out_shape=outs, in_specs=[vmem] * 3, out_sp...]
    pallas_call x1, Pallas kernels: 40.5 us -> 40 us  [tick(): pl.pallas_call(functools.partial(tick_kernel, n, per, experts, sections),...]
where the time goes in v3:
time: 41.6 us; the launch traced here: 41.4 us
  Pallas kernels  40.8 us (98%)
  between operations  0.64 us (2%)
    pallas_call x1, Pallas kernels, tick(): pl.pallas_call(functools.partial(tick_kernel, n, per, experts, sections),...  40 us

profile of v3, /device:TPU:0, one launch (start us, length us, event | category | flops | bytes accessed | tf_op | source)
XLA Modules:
  0.0 41.4 jit_solution(9965766849713943915)
XLA Ops:
  0.6 40.0 %shard_map.130 = (bf16[128,512]{1,0:T(8,128)(2,1)S(1)}, f32[64,512]{1,0:T(8,128)S(1)}, f32[64,512]{1,0:T(8,128)S(1)}) custom-call(bf16[128,512]{1,0:T(8,128)(2,1)} %bitcast.17, bf16[128,512]{1,0:T(8,128)(2,1)} %bitcast.18, s32[2,128]{1,0:T(2,128)} %bitcast.22, s32[1,4]{1,0:T(1,128)} %len_ref.1, f32[1,2048]{1,0:T(1,128)} %gain_ref.1, ...), custom_call_target="tpu_custom_call" | custom-call | tf_op jit(solution)/shard_map/pallas_call | solution.py:456
  40.7 0.8 %shard_map.131 = (bf16[128,512]{1,0:T(8,128)(2,1)}, f32[64,512]{1,0:T(8,128)}, f32[64,512]{1,0:T(8,128)}) custom-call(bf16[128,512]{1,0:T(8,128)(2,1)S(1)} %get-tuple-element.9.refs_0_, f32[64,512]{1,0:T(8,128)S(1)} %get-tuple-element.10.refs_1_, f32[64,512]{1,0:T(8,128)S(1)} %get-tuple-element.11.refs_2_), custom_call_target="tpu_custom_call" | custom-call | tf_op jit(solution)/shard_map/pallas_call | solution.py:508
